TPU v7x, 128 devices: a whole 4x4x4 slice. The times are simulated.
128 devices in a mesh: dp: 8 (over x, core), pipe: 4 (over y), tensor: 4 (over z).
Axes of the slice: x: 4, y: 4, z: 4, core: 2. Of those that a mesh axis runs over, the one named last changes fastest.
Arguments:
- support_tokens: int32 [64, 32], P(('dp', 'pipe')), may hold values from 0 to 64127
- support_lengths: int32 [64], P(('dp', 'pipe')), may hold values from 1 to 32
- support_labels: int32 [64, 1], P(('dp', 'pipe')), may hold values from 0 to 31
- query_tokens: int32 [32, 32], P(('dp', 'pipe')), may hold values from 0 to 64127
- query_lengths: int32 [32], P(('dp', 'pipe')), may hold values from 1 to 32
- query_episodes: int32 [32], P(('dp', 'pipe')), may hold values from 0 to 1
- embedding: bfloat16 [64128, 4096], P(('dp', 'pipe'), 'tensor'), may hold values from -18 to 18
- attn_gain: float32 [4, 4096], P('pipe'), may hold values from 0.5 to 1.5
- query_weight: bfloat16 [4, 4096, 4096], P('pipe', None, 'tensor'), may hold values from -1 to 1
- key_weight: bfloat16 [4, 4096, 1024], P('pipe', None, 'tensor'), may hold values from -16 to 16
- value_weight: bfloat16 [4, 4096, 1024], P('pipe', None, 'tensor'), may hold values from -0.09375 to 0.09375
- out_weight: bfloat16 [4, 4096, 4096], P('pipe', 'tensor'), may hold values from -0.09375 to 0.09375
- final_gain: float32 [4096], replicated, may hold values from 0.5 to 1.5
Outputs:
- prototypes: float32 [32, 4096], P(None, 'tensor')
- logits: float32 [32, 16], P(('dp', 'pipe'))
Inputs may be any that keep to these rules, and one draw needn't show every extreme that they name: `support_labels`: every class is the label of at least one support sequence.
All inputs are finite; a program needn't handle non-finite values.
Results may differ from a plain program's by a relative error of at most 0.024.
Values may be sent and summed in bfloat16 or wider, within the bound.
A program may use at most 128 MiB of HBM per device.

v0:
```python
import math
import jax
import jax.numpy as jnp
from jax import lax
from jax.sharding import PartitionSpec as P

D = 4096
HEAD_DIM = 128
WAYS = 16
EPISODES = 2
epsilon = 1e-05
rotary_base = 500000.0


def in_order(blocks, dim):
    blocks = jnp.moveaxis(blocks, 0, dim)
    dims = blocks.shape
    return blocks.reshape(*dims[:dim], dims[dim] * dims[dim + 1], *dims[dim + 2 :])


def sent_to_all(shard, axis):
    copies = jnp.broadcast_to(shard, (lax.axis_size(axis), *shard.shape))
    return lax.all_to_all(copies, axis, split_axis=0, concat_axis=0, tiled=True)


def collect(shard, axis, dim):
    return in_order(sent_to_all(shard, axis), dim)


def split_up(shard, dim, length):
    dims = shard.shape
    blocks = shard.reshape(*dims[:dim], length, dims[dim] // length, *dims[dim + 1 :])
    return jnp.moveaxis(blocks, dim, 0)


def sum_at_owner(shard, axis, dim):
    length = lax.axis_size(axis)
    blocks = lax.all_to_all(split_up(shard, dim, length), axis, 0, 0, tiled=True)
    return jnp.sum(blocks.astype(jnp.float32), axis=0)


def passed_along(block, axis, distance):
    devices = range(lax.axis_size(axis))
    route = [((i - distance) % len(devices), i) for i in devices]
    return lax.ppermute(block, axis, route)


def over_copies(shard, axis):
    return sent_to_all(shard, axis).astype(jnp.float32).sum(axis=0)


def rotate(heads_in, seq_len):
    half_dim = HEAD_DIM // 2
    freqs = jnp.exp(
        -math.log(rotary_base) * jnp.arange(half_dim, dtype=jnp.float32) * (2.0 / HEAD_DIM)
    )
    angles = jnp.arange(seq_len, dtype=jnp.float32)[:, None] * freqs[None, :]
    cosine = jnp.cos(angles)[None, :, None, :]
    sine = jnp.sin(angles)[None, :, None, :]
    first_half = heads_in[..., :half_dim]
    second_half = heads_in[..., half_dim:]
    return jnp.concatenate(
        [first_half * cosine - second_half * sine, second_half * cosine + first_half * sine],
        axis=-1,
    )


def whole_rows(hidden):
    return collect(hidden, "tensor", 1)


def whole_values(full_rows, gain_vector):
    values = full_rows.astype(jnp.float32)
    mean_square = jnp.mean(values * values, axis=-1, keepdims=True)
    return values * lax.rsqrt(mean_square + epsilon) * gain_vector


def shards(
    support_tokens,
    support_lengths,
    support_labels,
    query_tokens,
    query_lengths,
    query_episodes,
    embedding,
    attn_gain,
    query_weight,
    key_weight,
    value_weight,
    out_weight,
    final_gain,
):
    group_count = lax.axis_size(("dp", "pipe"))
    sections = lax.axis_size("pipe")
    sup_dev, seq_len = support_tokens.shape
    qry_dev = query_tokens.shape[0]
    seq_count = sup_dev + qry_dev
    row_count = seq_count * seq_len
    table_rows, width = embedding.shape
    column_start = lax.axis_index("tensor") * width
    all_support, all_query, every_sup_len, every_qry_len = (
        lax.all_gather(support_tokens, ("dp", "pipe"), axis=0, tiled=True),
        lax.all_gather(query_tokens, ("dp", "pipe"), axis=0, tiled=True),
        lax.all_gather(support_lengths, ("dp", "pipe"), axis=0, tiled=True),
        lax.all_gather(query_lengths, ("dp", "pipe"), axis=0, tiled=True),
    )
    token_flat = jnp.concatenate(
        [all_support.reshape(group_count, sup_dev * seq_len), all_query], axis=1
    ).reshape(group_count * row_count)
    local_ids = token_flat - lax.axis_index(("dp", "pipe")) * table_rows
    inside = (local_ids >= 0) & (local_ids < table_rows)
    picked = jnp.take(embedding, jnp.clip(local_ids, 0, table_rows - 1), axis=0)
    picked = jnp.where(inside[:, None], picked, jnp.zeros_like(picked))
    replies = lax.all_to_all(picked, ("dp", "pipe"), split_axis=0, concat_axis=0, tiled=True)
    hidden = jnp.sum(
        replies.reshape(group_count, row_count, width).astype(jnp.float32), axis=0
    ).astype(jnp.bfloat16)
    seq_lengths = jnp.concatenate([support_lengths, query_lengths], axis=0)
    query_proj = query_weight[0]
    key_proj = key_weight[0]
    value_proj = value_weight[0]
    out_proj = out_weight[0]
    gain_vector = attn_gain[0]
    local_heads = query_proj.shape[1] // HEAD_DIM
    local_groups = key_proj.shape[1] // HEAD_DIM
    group_size = local_heads // local_groups
    w_in = jnp.concatenate([query_proj, key_proj, value_proj], axis=1)
    query_cols = local_heads * HEAD_DIM
    key_cols = local_groups * HEAD_DIM
    positions = jnp.arange(seq_len)
    causal = positions[None, :] <= positions[:, None]

    def section_block(stream, lengths_here):
        normed = whole_values(whole_rows(stream), gain_vector).astype(jnp.bfloat16)
        projected = jnp.dot(normed, w_in, preferred_element_type=jnp.float32)
        query_heads = projected[:, :query_cols].reshape(seq_count, seq_len, local_heads, HEAD_DIM)
        key_heads = projected[:, query_cols : query_cols + key_cols].reshape(
            seq_count, seq_len, local_groups, HEAD_DIM
        )
        value_heads = (
            projected[:, query_cols + key_cols :]
            .reshape(seq_count, seq_len, local_groups, HEAD_DIM)
            .astype(jnp.bfloat16)
        )
        query_heads = (
            rotate(query_heads, seq_len)
            .astype(jnp.bfloat16)
            .reshape(seq_count, seq_len, local_groups, group_size, HEAD_DIM)
        )
        key_heads = rotate(key_heads, seq_len).astype(jnp.bfloat16)
        scores = jnp.einsum(
            "sikgd,sjkd->skgij", query_heads, key_heads, preferred_element_type=jnp.float32
        ) / math.sqrt(HEAD_DIM)
        visible = causal[None, :, :] & (positions[None, None, :] < lengths_here[:, None, None])
        scores = jnp.where(visible[:, None, None, :, :], scores, -1e30)
        weights = jax.nn.softmax(scores, axis=-1).astype(jnp.bfloat16)
        mixed = jnp.einsum(
            "skgij,sjkd->sikgd", weights, value_heads, preferred_element_type=jnp.float32
        )
        mixed = mixed.astype(jnp.bfloat16).reshape(row_count, query_cols)
        partial_out = jnp.dot(mixed, out_proj, preferred_element_type=jnp.float32)
        summed = sum_at_owner(partial_out.astype(jnp.bfloat16), "tensor", 1)
        return (stream.astype(jnp.float32) + summed).astype(jnp.bfloat16)

    section_index = lax.axis_index("pipe")
    dp_base = lax.axis_index("dp") * sections

    def tick(tick_index, stream):
        held_group = dp_base + (section_index - tick_index) % sections
        sup_part = lax.dynamic_slice_in_dim(every_sup_len, held_group * sup_dev, sup_dev)
        qry_part = lax.dynamic_slice_in_dim(every_qry_len, held_group * qry_dev, qry_dev)
        lengths_here = jnp.concatenate([sup_part, qry_part], axis=0)
        first_tick = (tick_index - section_index) % sections
        active = (first_tick <= tick_index) & (tick_index < first_tick + sections)
        computed = section_block(stream, lengths_here)
        stream = jnp.where(active, computed, stream)
        return passed_along(stream, "pipe", 1)

    hidden = lax.fori_loop(0, 2 * sections, tick, hidden)
    final = lax.dynamic_slice_in_dim(
        whole_values(whole_rows(hidden), final_gain), column_start, width, 1
    )
    live = (positions[None, :] < seq_lengths[:, None]).astype(jnp.float32)
    pooled = jnp.sum(
        final.reshape(seq_count, seq_len, width) * live[:, :, None], axis=1
    ) / seq_lengths[:, None].astype(jnp.float32)
    support_pooled = pooled[:sup_dev]
    query_pooled = pooled[sup_dev:]
    class_count_all = EPISODES * WAYS
    onehot = (support_labels[:, 0][:, None] == jnp.arange(class_count_all)[None, :]).astype(
        jnp.float32
    )
    class_total = jnp.dot(onehot.T, support_pooled, precision=lax.Precision.HIGHEST)
    class_count = jnp.sum(onehot, axis=0)
    class_total, class_count = (
        over_copies(class_total.astype(jnp.bfloat16), ("dp", "pipe")).astype(jnp.float32),
        over_copies(class_count.astype(jnp.bfloat16), ("dp", "pipe")).astype(jnp.float32),
    )
    prototypes = class_total / class_count[:, None]
    episode_pick = (query_episodes[:, None] == jnp.arange(EPISODES)[None, :]).astype(jnp.float32)
    chosen = jnp.einsum(
        "qe,ewc->qwc",
        episode_pick,
        prototypes.reshape(EPISODES, WAYS, width),
        precision=lax.Precision.HIGHEST,
    )
    partial_distance = jnp.sum((query_pooled[:, None, :] - chosen) ** 2, axis=-1)
    distance = lax.psum(partial_distance, "tensor")
    logits = -distance / math.sqrt(D)
    return (prototypes, logits)


def solution(mesh):
    return jax.shard_map(
        shards,
        mesh=mesh,
        in_specs=(
            P(("dp", "pipe"), None),
            P(("dp", "pipe")),
            P(("dp", "pipe"), None),
            P(("dp", "pipe"), None),
            P(("dp", "pipe")),
            P(("dp", "pipe")),
            P(("dp", "pipe"), "tensor"),
            P("pipe", None),
            P("pipe", None, "tensor"),
            P("pipe", None, "tensor"),
            P("pipe", None, "tensor"),
            P("pipe", "tensor", None),
            P(),
        ),
        out_specs=(P(None, "tensor"), P(("dp", "pipe"), None)),
        check_vma=False,
    )
```

profile of v0, /device:TPU:0, one launch (start us, length us, event | category | flops | bytes accessed | tf_op | source)
XLA Modules:
  0.0 681.9 jit_solution(12424556584828293104)
XLA Ops:
  0.6 33.8 %all-gather.1 = s32[32,1,32]{2,1,0:T(1,128)S(1)} all-gather(s32[1,1,32]{2,1,0:T(1,128)} %bitcast.148), channel_id=1, replica_groups=mesh['dp'=8,'pipe'=4,'tensor'=4] {'dp','pipe'}, dimensions={0}, use_global_device_ids=true | all-gather | bytes 4224 | tf_op jit(solution)/shard_map/all_gather | solution.py:103
  34.4 36.5 %all-gather = s32[32,2,32]{2,1,0:T(2,128)S(1)} all-gather(s32[1,2,32]{2,1,0:T(2,128)} %bitcast.144), channel_id=1, replica_groups=mesh['dp'=8,'pipe'=4,'tensor'=4] {'dp','pipe'}, dimensions={0}, use_global_device_ids=true | all-gather | bytes 8448 | tf_op jit(solution)/shard_map/all_gather | solution.py:102
  71.2 18.7 %gather_fusion = bf16[3072,1024]{1,0:T(8,128)(2,1)} fusion(bf16[2004,1024]{1,0:T(8,128)(2,1)} %param.21, s32[3072]{0:T(1024)S(1)} %broadcast_clamp_fusion.1), kind=kCustom, calls=%fused_computation | custom fusion | bytes 12595200 | tf_op jit(solution)/shard_map/jit(_take)/gather | solution.py:112
  89.9 7.0 %select_select_fusion = bf16[32,96,1024]{2,1,0:T(8,128)(2,1)} fusion(bf16[32,96,1024]{2,1,0:T(8,128)(2,1)} %bitcast.128, pred[32,96]{1,0:T(8,128)(4,1)S(1)} %get-tuple-element.312, pred[32,96]{1,0:T(8,128)(4,1)S(1)} %get-tuple-element.322), kind=kLoop, calls=%fused_computation.56 | loop fusion | flops 6291456 | bytes 12589056 | tf_op jit(solution)/shard_map/jit(_where)/select_n | solution.py:113
  105.7 79.5 %all-reduce.2 = (s32[64]{0:T(128)S(1)}, s32[32]{0:T(128)S(1)}) all-reduce(s32[64]{0:T(128)S(1)} %dynamic-update-slice, s32[32]{0:T(128)S(1)} %dynamic-update-slice.1), channel_id=1, replica_groups=mesh['dp'=8,'pipe'=4,'tensor'=4] {'dp','pipe'}, use_global_device_ids=true, to_apply=%add | all-reduce | flops 96 | bytes 768
  185.3 11.6 %pad_maximum_fusion = bf16[4096,1536]{1,0:T(8,128)(2,1)} fusion(bf16[4096,256]{1,0:T(8,128)(2,1)S(1)} %bitcast.135, bf16[4096,256]{1,0:T(8,128)(2,1)} %bitcast.136, bf16[4096,1024]{1,0:T(8,128)(2,1)} %bitcast.129), kind=kLoop, calls=%fused_computation.55 | loop fusion | flops 37748736 | bytes 25165824 | tf_op jit(solution)/shard_map/concatenate | solution.py:127
  201.1 409.0 %while.16 = (s32[]{:T(128)}, bf16[96,1024]{1,0:T(8,128)(2,1)S(1)}, s32[]{:T(128)}, f32[1,4096]{1,0:T(1,128)S(1)}, bf16[4096,1536]{1,0:T(8,128)(2,1)}, /*index=5*...) while((s32[]{:T(128)}, bf16[96,1024]{1,0:T(8,128)(2,1)S(1)}, ...), condition=%wide.region_6.7_spmd.clone, body=%wide.region_1.0_spmd.clone.sunk | while | flops 2038168704 | bytes 45535072 | solution.py:179
  209.2 10.1 %all-to-all-done = bf16[4,96,1024]{2,1,0:T(8,128)(2,1)S(1)} async-done(((bf16[4,96,1024]{2,1,0:T(8,128)(2,1)}), bf16[4,96,1024]{2,1,0:T(8,128)(2,1)S(1)}, u32[]{:S(2)}, u32[]{:S(2)}) %all-to-all-start) | async-done | bytes 786464 | tf_op jit(solution)/shard_map/while/body/eval_jaxpr/all_to_all | solution.py:23
  238.3 11.0 %all-to-all-done.1 = bf16[4,96,1024]{2,1,0:T(8,128)(2,1)S(1)} async-done(((bf16[4,96,1024]{2,1,0:T(8,128)(2,1)}), bf16[4,96,1024]{2,1,0:T(8,128)(2,1)S(1)}, u32[]{:S(2)}, u32[]{:S(2)}) %all-to-all-start.1) | async-done | bytes 786464 | tf_op jit(solution)/shard_map/while/body/eval_jaxpr/all_to_all | solution.py:38
  262.7 7.7 %all-to-all-done = bf16[4,96,1024]{2,1,0:T(8,128)(2,1)S(1)} async-done(((bf16[4,96,1024]{2,1,0:T(8,128)(2,1)}), bf16[4,96,1024]{2,1,0:T(8,128)(2,1)S(1)}, u32[]{:S(2)}, u32[]{:S(2)}) %all-to-all-start) | async-done | bytes 786464 | tf_op jit(solution)/shard_map/while/body/eval_jaxpr/all_to_all | solution.py:23
  289.3 9.4 %all-to-all-done.1 = bf16[4,96,1024]{2,1,0:T(8,128)(2,1)S(1)} async-done(((bf16[4,96,1024]{2,1,0:T(8,128)(2,1)}), bf16[4,96,1024]{2,1,0:T(8,128)(2,1)S(1)}, u32[]{:S(2)}, u32[]{:S(2)}) %all-to-all-start.1) | async-done | bytes 786464 | tf_op jit(solution)/shard_map/while/body/eval_jaxpr/all_to_all | solution.py:38
  299.0 6.9 %collective-permute-done = bf16[96,1024]{1,0:T(8,128)(2,1)S(1)} collective-permute-done((bf16[96,1024]{1,0:T(8,128)(2,1)S(1)}, bf16[96,1024]{1,0:T(8,128)(2,1)S(1)}, u32[]{:S(2)}, u32[]{:S(2)}) %collective-permute-start) | collective-permute-done | bytes 196640 | tf_op jit(solution)/shard_map/while/body/eval_jaxpr/ppermute | solution.py:45
  312.2 7.7 %all-to-all-done = bf16[4,96,1024]{2,1,0:T(8,128)(2,1)S(1)} async-done(((bf16[4,96,1024]{2,1,0:T(8,128)(2,1)}), bf16[4,96,1024]{2,1,0:T(8,128)(2,1)S(1)}, u32[]{:S(2)}, u32[]{:S(2)}) %all-to-all-start) | async-done | bytes 786464 | tf_op jit(solution)/shard_map/while/body/eval_jaxpr/all_to_all | solution.py:23
  338.8 9.4 %all-to-all-done.1 = bf16[4,96,1024]{2,1,0:T(8,128)(2,1)S(1)} async-done(((bf16[4,96,1024]{2,1,0:T(8,128)(2,1)}), bf16[4,96,1024]{2,1,0:T(8,128)(2,1)S(1)}, u32[]{:S(2)}, u32[]{:S(2)}) %all-to-all-start.1) | async-done | bytes 786464 | tf_op jit(solution)/shard_map/while/body/eval_jaxpr/all_to_all | solution.py:38
  348.5 6.9 %collective-permute-done = bf16[96,1024]{1,0:T(8,128)(2,1)S(1)} collective-permute-done((bf16[96,1024]{1,0:T(8,128)(2,1)S(1)}, bf16[96,1024]{1,0:T(8,128)(2,1)S(1)}, u32[]{:S(2)}, u32[]{:S(2)}) %collective-permute-start) | collective-permute-done | bytes 196640 | tf_op jit(solution)/shard_map/while/body/eval_jaxpr/ppermute | solution.py:45
  361.7 7.7 %all-to-all-done = bf16[4,96,1024]{2,1,0:T(8,128)(2,1)S(1)} async-done(((bf16[4,96,1024]{2,1,0:T(8,128)(2,1)}), bf16[4,96,1024]{2,1,0:T(8,128)(2,1)S(1)}, u32[]{:S(2)}, u32[]{:S(2)}) %all-to-all-start) | async-done | bytes 786464 | tf_op jit(solution)/shard_map/while/body/eval_jaxpr/all_to_all | solution.py:23
  388.3 9.4 %all-to-all-done.1 = bf16[4,96,1024]{2,1,0:T(8,128)(2,1)S(1)} async-done(((bf16[4,96,1024]{2,1,0:T(8,128)(2,1)}), bf16[4,96,1024]{2,1,0:T(8,128)(2,1)S(1)}, u32[]{:S(2)}, u32[]{:S(2)}) %all-to-all-start.1) | async-done | bytes 786464 | tf_op jit(solution)/shard_map/while/body/eval_jaxpr/all_to_all | solution.py:38
  398.0 6.9 %collective-permute-done = bf16[96,1024]{1,0:T(8,128)(2,1)S(1)} collective-permute-done((bf16[96,1024]{1,0:T(8,128)(2,1)S(1)}, bf16[96,1024]{1,0:T(8,128)(2,1)S(1)}, u32[]{:S(2)}, u32[]{:S(2)}) %collective-permute-start) | collective-permute-done | bytes 196640 | tf_op jit(solution)/shard_map/while/body/eval_jaxpr/ppermute | solution.py:45
  411.2 7.7 %all-to-all-done = bf16[4,96,1024]{2,1,0:T(8,128)(2,1)S(1)} async-done(((bf16[4,96,1024]{2,1,0:T(8,128)(2,1)}), bf16[4,96,1024]{2,1,0:T(8,128)(2,1)S(1)}, u32[]{:S(2)}, u32[]{:S(2)}) %all-to-all-start) | async-done | bytes 786464 | tf_op jit(solution)/shard_map/while/body/eval_jaxpr/all_to_all | solution.py:23
  437.8 10.7 %all-to-all-done.1 = bf16[4,96,1024]{2,1,0:T(8,128)(2,1)S(1)} async-done(((bf16[4,96,1024]{2,1,0:T(8,128)(2,1)}), bf16[4,96,1024]{2,1,0:T(8,128)(2,1)S(1)}, u32[]{:S(2)}, u32[]{:S(2)}) %all-to-all-start.1) | async-done | bytes 786464 | tf_op jit(solution)/shard_map/while/body/eval_jaxpr/all_to_all | solution.py:38
  462.0 7.7 %all-to-all-done = bf16[4,96,1024]{2,1,0:T(8,128)(2,1)S(1)} async-done(((bf16[4,96,1024]{2,1,0:T(8,128)(2,1)}), bf16[4,96,1024]{2,1,0:T(8,128)(2,1)S(1)}, u32[]{:S(2)}, u32[]{:S(2)}) %all-to-all-start) | async-done | bytes 786464 | tf_op jit(solution)/shard_map/while/body/eval_jaxpr/all_to_all | solution.py:23
  488.6 13.1 %all-to-all-done.1 = bf16[4,96,1024]{2,1,0:T(8,128)(2,1)S(1)} async-done(((bf16[4,96,1024]{2,1,0:T(8,128)(2,1)}), bf16[4,96,1024]{2,1,0:T(8,128)(2,1)S(1)}, u32[]{:S(2)}, u32[]{:S(2)}) %all-to-all-start.1) | async-done | bytes 786464 | tf_op jit(solution)/shard_map/while/body/eval_jaxpr/all_to_all | solution.py:38
  502.0 6.9 %collective-permute-done = bf16[96,1024]{1,0:T(8,128)(2,1)S(1)} collective-permute-done((bf16[96,1024]{1,0:T(8,128)(2,1)S(1)}, bf16[96,1024]{1,0:T(8,128)(2,1)S(1)}, u32[]{:S(2)}, u32[]{:S(2)}) %collective-permute-start) | collective-permute-done | bytes 196640 | tf_op jit(solution)/shard_map/while/body/eval_jaxpr/ppermute | solution.py:45
  515.1 7.7 %all-to-all-done = bf16[4,96,1024]{2,1,0:T(8,128)(2,1)S(1)} async-done(((bf16[4,96,1024]{2,1,0:T(8,128)(2,1)}), bf16[4,96,1024]{2,1,0:T(8,128)(2,1)S(1)}, u32[]{:S(2)}, u32[]{:S(2)}) %all-to-all-start) | async-done | bytes 786464 | tf_op jit(solution)/shard_map/while/body/eval_jaxpr/all_to_all | solution.py:23
  541.8 10.0 %all-to-all-done.1 = bf16[4,96,1024]{2,1,0:T(8,128)(2,1)S(1)} async-done(((bf16[4,96,1024]{2,1,0:T(8,128)(2,1)}), bf16[4,96,1024]{2,1,0:T(8,128)(2,1)S(1)}, u32[]{:S(2)}, u32[]{:S(2)}) %all-to-all-start.1) | async-done | bytes 786464 | tf_op jit(solution)/shard_map/while/body/eval_jaxpr/all_to_all | solution.py:38
  552.0 6.9 %collective-permute-done = bf16[96,1024]{1,0:T(8,128)(2,1)S(1)} collective-permute-done((bf16[96,1024]{1,0:T(8,128)(2,1)S(1)}, bf16[96,1024]{1,0:T(8,128)(2,1)S(1)}, u32[]{:S(2)}, u32[]{:S(2)}) %collective-permute-start) | collective-permute-done | bytes 196640 | tf_op jit(solution)/shard_map/while/body/eval_jaxpr/ppermute | solution.py:45
  565.2 9.5 %all-to-all-done = bf16[4,96,1024]{2,1,0:T(8,128)(2,1)S(1)} async-done(((bf16[4,96,1024]{2,1,0:T(8,128)(2,1)}), bf16[4,96,1024]{2,1,0:T(8,128)(2,1)S(1)}, u32[]{:S(2)}, u32[]{:S(2)}) %all-to-all-start) | async-done | bytes 786464 | tf_op jit(solution)/shard_map/while/body/eval_jaxpr/all_to_all | solution.py:23
  593.6 9.4 %all-to-all-done.1 = bf16[4,96,1024]{2,1,0:T(8,128)(2,1)S(1)} async-done(((bf16[4,96,1024]{2,1,0:T(8,128)(2,1)}), bf16[4,96,1024]{2,1,0:T(8,128)(2,1)S(1)}, u32[]{:S(2)}, u32[]{:S(2)}) %all-to-all-start.1) | async-done | bytes 786464 | tf_op jit(solution)/shard_map/while/body/eval_jaxpr/all_to_all | solution.py:38
  603.3 6.9 %collective-permute-done = bf16[96,1024]{1,0:T(8,128)(2,1)S(1)} collective-permute-done((bf16[96,1024]{1,0:T(8,128)(2,1)S(1)}, bf16[96,1024]{1,0:T(8,128)(2,1)S(1)}, u32[]{:S(2)}, u32[]{:S(2)}) %collective-permute-start) | collective-permute-done | bytes 196640 | tf_op jit(solution)/shard_map/while/body/eval_jaxpr/ppermute | solution.py:45
  614.9 9.2 %all-to-all-done.3 = bf16[4,96,1024]{2,1,0:T(8,128)(2,1)S(1)} async-done(((bf16[4,96,1024]{2,1,0:T(8,128)(2,1)}), bf16[4,96,1024]{2,1,0:T(8,128)(2,1)S(1)}, u32[]{:S(2)}, u32[]{:S(2)}) %all-to-all-start.3) | async-done | bytes 786464 | tf_op jit(solution)/shard_map/all_to_all | solution.py:23
  643.8 27.6 %all-to-all-done.4 = bf16[32,32,1024]{2,1,0:T(8,128)(2,1)S(1)} async-done(((bf16[32,32,1024]{2,1,0:T(8,128)(2,1)}), bf16[32,32,1024]{2,1,0:T(8,128)(2,1)S(1)}, u32[]{:S(2)}, u32[]{:S(2)}) %all-to-all-start.4) | async-done | bytes 2097184 | tf_op jit(solution)/shard_map/all_to_all | solution.py:23
  672.4 8.9 %psum.7 = f32[1,16]{1,0:T(1,128)S(1)} all-reduce(f32[1,16]{1,0:T(1,128)S(1)} %bitcast.147), channel_id=1, replica_groups=mesh['dp'=8,'pipe'=4,'tensor'=4] {'tensor'}, use_global_device_ids=true, to_apply=%region_13.14 | all-reduce | flops 16 | bytes 128 | tf_op jit(solution)/shard_map/psum | solution.py:208
  (342 shorter events, 255.2 us)
Async XLA Ops:
  96.9 88.4 %copy-start = (bf16[1,4096,256]{2,1,0:T(8,128)(2,1)S(1)}, bf16[1,4096,256]{2,1,0:T(8,128)(2,1)}, u32[]{:S(2)}) copy-start(bf16[1,4096,256]{2,1,0:T(8,128)(2,1)} %param.25) | copy-start | bytes 6291460
  96.9 99.9 %all-to-all-start.2 = ((bf16[32,96,1024]{2,1,0:T(8,128)(2,1)}), bf16[32,96,1024]{2,1,0:T(8,128)(2,1)}, u32[]{:S(2)}, u32[]{:S(2)}) async-start(bf16[32,96,1024]{2,1,0:T(8,128)(2,1)} %select_select_fusion), calls=%async_computation.2 | async-start | bytes 12582912 | tf_op jit(solution)/shard_map/all_to_all | solution.py:114
  201.1 413.6 %copy-start.3 = (s32[2,1]{0,1:T(1,128)S(1)}, s32[2,1]{0,1:T(1,128)}, u32[]{:S(2)}) copy-start(s32[2,1]{0,1:T(1,128)} %param.17) | copy-start | bytes 28
  202.2 17.2 %all-to-all-start = ((bf16[4,96,1024]{2,1,0:T(8,128)(2,1)}), bf16[4,96,1024]{2,1,0:T(8,128)(2,1)S(1)}, u32[]{:S(2)}, u32[]{:S(2)}) async-start(bf16[4,96,1024]{2,1,0:T(8,128)(2,1)} %broadcast_in_dim.169), calls=%async_computation | async-start | bytes 1572864 | tf_op jit(solution)/shard_map/while/body/eval_jaxpr/all_to_all | solution.py:23
  234.8 14.5 %all-to-all-start.1 = ((bf16[4,96,1024]{2,1,0:T(8,128)(2,1)}), bf16[4,96,1024]{2,1,0:T(8,128)(2,1)S(1)}, u32[]{:S(2)}, u32[]{:S(2)}) async-start(bf16[4,96,1024]{2,1,0:T(8,128)(2,1)} %bitcast.122), calls=%async_computation.1 | async-start | bytes 1572864 | tf_op jit(solution)/shard_map/while/body/eval_jaxpr/all_to_all | solution.py:38
  249.5 6.9 %collective-permute-start = (bf16[96,1024]{1,0:T(8,128)(2,1)S(1)}, bf16[96,1024]{1,0:T(8,128)(2,1)S(1)}, u32[]{:S(2)}, u32[]{:S(2)}) collective-permute-start(bf16[96,1024]{1,0:T(8,128)(2,1)S(1)} %fusion.89), channel_id=1, source_target_pairs={{12,0},{0,4},{4,8},{8,12},{13,1},{1,5},{5,9},{9,13},{14,2},{2,6},{... | collective-permute-start | bytes 589832 | tf_op jit(solution)/shard_map/while/body/eval_jaxpr/ppermute | solution.py:45
  257.4 13.0 %all-to-all-start = ((bf16[4,96,1024]{2,1,0:T(8,128)(2,1)}), bf16[4,96,1024]{2,1,0:T(8,128)(2,1)S(1)}, u32[]{:S(2)}, u32[]{:S(2)}) async-start(bf16[4,96,1024]{2,1,0:T(8,128)(2,1)} %broadcast_in_dim.169), calls=%async_computation | async-start | bytes 1572864 | tf_op jit(solution)/shard_map/while/body/eval_jaxpr/all_to_all | solution.py:23
  285.8 13.0 %all-to-all-start.1 = ((bf16[4,96,1024]{2,1,0:T(8,128)(2,1)}), bf16[4,96,1024]{2,1,0:T(8,128)(2,1)S(1)}, u32[]{:S(2)}, u32[]{:S(2)}) async-start(bf16[4,96,1024]{2,1,0:T(8,128)(2,1)} %bitcast.122), calls=%async_computation.1 | async-start | bytes 1572864 | tf_op jit(solution)/shard_map/while/body/eval_jaxpr/all_to_all | solution.py:38
  299.0 6.9 %collective-permute-start = (bf16[96,1024]{1,0:T(8,128)(2,1)S(1)}, bf16[96,1024]{1,0:T(8,128)(2,1)S(1)}, u32[]{:S(2)}, u32[]{:S(2)}) collective-permute-start(bf16[96,1024]{1,0:T(8,128)(2,1)S(1)} %fusion.89), channel_id=1, source_target_pairs={{12,0},{0,4},{4,8},{8,12},{13,1},{1,5},{5,9},{9,13},{14,2},{2,6},{... | collective-permute-start | bytes 589832 | tf_op jit(solution)/shard_map/while/body/eval_jaxpr/ppermute | solution.py:45
  306.9 13.0 %all-to-all-start = ((bf16[4,96,1024]{2,1,0:T(8,128)(2,1)}), bf16[4,96,1024]{2,1,0:T(8,128)(2,1)S(1)}, u32[]{:S(2)}, u32[]{:S(2)}) async-start(bf16[4,96,1024]{2,1,0:T(8,128)(2,1)} %broadcast_in_dim.169), calls=%async_computation | async-start | bytes 1572864 | tf_op jit(solution)/shard_map/while/body/eval_jaxpr/all_to_all | solution.py:23
  335.3 13.0 %all-to-all-start.1 = ((bf16[4,96,1024]{2,1,0:T(8,128)(2,1)}), bf16[4,96,1024]{2,1,0:T(8,128)(2,1)S(1)}, u32[]{:S(2)}, u32[]{:S(2)}) async-start(bf16[4,96,1024]{2,1,0:T(8,128)(2,1)} %bitcast.122), calls=%async_computation.1 | async-start | bytes 1572864 | tf_op jit(solution)/shard_map/while/body/eval_jaxpr/all_to_all | solution.py:38
  348.5 6.9 %collective-permute-start = (bf16[96,1024]{1,0:T(8,128)(2,1)S(1)}, bf16[96,1024]{1,0:T(8,128)(2,1)S(1)}, u32[]{:S(2)}, u32[]{:S(2)}) collective-permute-start(bf16[96,1024]{1,0:T(8,128)(2,1)S(1)} %fusion.89), channel_id=1, source_target_pairs={{12,0},{0,4},{4,8},{8,12},{13,1},{1,5},{5,9},{9,13},{14,2},{2,6},{... | collective-permute-start | bytes 589832 | tf_op jit(solution)/shard_map/while/body/eval_jaxpr/ppermute | solution.py:45
  356.4 13.0 %all-to-all-start = ((bf16[4,96,1024]{2,1,0:T(8,128)(2,1)}), bf16[4,96,1024]{2,1,0:T(8,128)(2,1)S(1)}, u32[]{:S(2)}, u32[]{:S(2)}) async-start(bf16[4,96,1024]{2,1,0:T(8,128)(2,1)} %broadcast_in_dim.169), calls=%async_computation | async-start | bytes 1572864 | tf_op jit(solution)/shard_map/while/body/eval_jaxpr/all_to_all | solution.py:23
  384.8 13.0 %all-to-all-start.1 = ((bf16[4,96,1024]{2,1,0:T(8,128)(2,1)}), bf16[4,96,1024]{2,1,0:T(8,128)(2,1)S(1)}, u32[]{:S(2)}, u32[]{:S(2)}) async-start(bf16[4,96,1024]{2,1,0:T(8,128)(2,1)} %bitcast.122), calls=%async_computation.1 | async-start | bytes 1572864 | tf_op jit(solution)/shard_map/while/body/eval_jaxpr/all_to_all | solution.py:38
  397.9 6.9 %collective-permute-start = (bf16[96,1024]{1,0:T(8,128)(2,1)S(1)}, bf16[96,1024]{1,0:T(8,128)(2,1)S(1)}, u32[]{:S(2)}, u32[]{:S(2)}) collective-permute-start(bf16[96,1024]{1,0:T(8,128)(2,1)S(1)} %fusion.89), channel_id=1, source_target_pairs={{12,0},{0,4},{4,8},{8,12},{13,1},{1,5},{5,9},{9,13},{14,2},{2,6},{... | collective-permute-start | bytes 589832 | tf_op jit(solution)/shard_map/while/body/eval_jaxpr/ppermute | solution.py:45
  405.9 13.0 %all-to-all-start = ((bf16[4,96,1024]{2,1,0:T(8,128)(2,1)}), bf16[4,96,1024]{2,1,0:T(8,128)(2,1)S(1)}, u32[]{:S(2)}, u32[]{:S(2)}) async-start(bf16[4,96,1024]{2,1,0:T(8,128)(2,1)} %broadcast_in_dim.169), calls=%async_computation | async-start | bytes 1572864 | tf_op jit(solution)/shard_map/while/body/eval_jaxpr/all_to_all | solution.py:23
  434.3 14.2 %all-to-all-start.1 = ((bf16[4,96,1024]{2,1,0:T(8,128)(2,1)}), bf16[4,96,1024]{2,1,0:T(8,128)(2,1)S(1)}, u32[]{:S(2)}, u32[]{:S(2)}) async-start(bf16[4,96,1024]{2,1,0:T(8,128)(2,1)} %bitcast.122), calls=%async_computation.1 | async-start | bytes 1572864 | tf_op jit(solution)/shard_map/while/body/eval_jaxpr/all_to_all | solution.py:38
  448.7 6.9 %collective-permute-start = (bf16[96,1024]{1,0:T(8,128)(2,1)S(1)}, bf16[96,1024]{1,0:T(8,128)(2,1)S(1)}, u32[]{:S(2)}, u32[]{:S(2)}) collective-permute-start(bf16[96,1024]{1,0:T(8,128)(2,1)S(1)} %fusion.89), channel_id=1, source_target_pairs={{12,0},{0,4},{4,8},{8,12},{13,1},{1,5},{5,9},{9,13},{14,2},{2,6},{... | collective-permute-start | bytes 589832 | tf_op jit(solution)/shard_map/while/body/eval_jaxpr/ppermute | solution.py:45
  456.7 13.0 %all-to-all-start = ((bf16[4,96,1024]{2,1,0:T(8,128)(2,1)}), bf16[4,96,1024]{2,1,0:T(8,128)(2,1)S(1)}, u32[]{:S(2)}, u32[]{:S(2)}) async-start(bf16[4,96,1024]{2,1,0:T(8,128)(2,1)} %broadcast_in_dim.169), calls=%async_computation | async-start | bytes 1572864 | tf_op jit(solution)/shard_map/while/body/eval_jaxpr/all_to_all | solution.py:23
  485.0 16.7 %all-to-all-start.1 = ((bf16[4,96,1024]{2,1,0:T(8,128)(2,1)}), bf16[4,96,1024]{2,1,0:T(8,128)(2,1)S(1)}, u32[]{:S(2)}, u32[]{:S(2)}) async-start(bf16[4,96,1024]{2,1,0:T(8,128)(2,1)} %bitcast.122), calls=%async_computation.1 | async-start | bytes 1572864 | tf_op jit(solution)/shard_map/while/body/eval_jaxpr/all_to_all | solution.py:38
  501.9 6.9 %collective-permute-start = (bf16[96,1024]{1,0:T(8,128)(2,1)S(1)}, bf16[96,1024]{1,0:T(8,128)(2,1)S(1)}, u32[]{:S(2)}, u32[]{:S(2)}) collective-permute-start(bf16[96,1024]{1,0:T(8,128)(2,1)S(1)} %fusion.89), channel_id=1, source_target_pairs={{12,0},{0,4},{4,8},{8,12},{13,1},{1,5},{5,9},{9,13},{14,2},{2,6},{... | collective-permute-start | bytes 589832 | tf_op jit(solution)/shard_map/while/body/eval_jaxpr/ppermute | solution.py:45
  509.9 13.0 %all-to-all-start = ((bf16[4,96,1024]{2,1,0:T(8,128)(2,1)}), bf16[4,96,1024]{2,1,0:T(8,128)(2,1)S(1)}, u32[]{:S(2)}, u32[]{:S(2)}) async-start(bf16[4,96,1024]{2,1,0:T(8,128)(2,1)} %broadcast_in_dim.169), calls=%async_computation | async-start | bytes 1572864 | tf_op jit(solution)/shard_map/while/body/eval_jaxpr/all_to_all | solution.py:23
  538.2 13.5 %all-to-all-start.1 = ((bf16[4,96,1024]{2,1,0:T(8,128)(2,1)}), bf16[4,96,1024]{2,1,0:T(8,128)(2,1)S(1)}, u32[]{:S(2)}, u32[]{:S(2)}) async-start(bf16[4,96,1024]{2,1,0:T(8,128)(2,1)} %bitcast.122), calls=%async_computation.1 | async-start | bytes 1572864 | tf_op jit(solution)/shard_map/while/body/eval_jaxpr/all_to_all | solution.py:38
  551.9 6.9 %collective-permute-start = (bf16[96,1024]{1,0:T(8,128)(2,1)S(1)}, bf16[96,1024]{1,0:T(8,128)(2,1)S(1)}, u32[]{:S(2)}, u32[]{:S(2)}) collective-permute-start(bf16[96,1024]{1,0:T(8,128)(2,1)S(1)} %fusion.89), channel_id=1, source_target_pairs={{12,0},{0,4},{4,8},{8,12},{13,1},{1,5},{5,9},{9,13},{14,2},{2,6},{... | collective-permute-start | bytes 589832 | tf_op jit(solution)/shard_map/while/body/eval_jaxpr/ppermute | solution.py:45
  559.9 14.7 %all-to-all-start = ((bf16[4,96,1024]{2,1,0:T(8,128)(2,1)}), bf16[4,96,1024]{2,1,0:T(8,128)(2,1)S(1)}, u32[]{:S(2)}, u32[]{:S(2)}) async-start(bf16[4,96,1024]{2,1,0:T(8,128)(2,1)} %broadcast_in_dim.169), calls=%async_computation | async-start | bytes 1572864 | tf_op jit(solution)/shard_map/while/body/eval_jaxpr/all_to_all | solution.py:23
  590.0 13.0 %all-to-all-start.1 = ((bf16[4,96,1024]{2,1,0:T(8,128)(2,1)}), bf16[4,96,1024]{2,1,0:T(8,128)(2,1)S(1)}, u32[]{:S(2)}, u32[]{:S(2)}) async-start(bf16[4,96,1024]{2,1,0:T(8,128)(2,1)} %bitcast.122), calls=%async_computation.1 | async-start | bytes 1572864 | tf_op jit(solution)/shard_map/while/body/eval_jaxpr/all_to_all | solution.py:38
  603.2 6.9 %collective-permute-start = (bf16[96,1024]{1,0:T(8,128)(2,1)S(1)}, bf16[96,1024]{1,0:T(8,128)(2,1)S(1)}, u32[]{:S(2)}, u32[]{:S(2)}) collective-permute-start(bf16[96,1024]{1,0:T(8,128)(2,1)S(1)} %fusion.89), channel_id=1, source_target_pairs={{12,0},{0,4},{4,8},{8,12},{13,1},{1,5},{5,9},{9,13},{14,2},{2,6},{... | collective-permute-start | bytes 589832 | tf_op jit(solution)/shard_map/while/body/eval_jaxpr/ppermute | solution.py:45
  611.1 13.0 %all-to-all-start.3 = ((bf16[4,96,1024]{2,1,0:T(8,128)(2,1)}), bf16[4,96,1024]{2,1,0:T(8,128)(2,1)S(1)}, u32[]{:S(2)}, u32[]{:S(2)}) async-start(bf16[4,96,1024]{2,1,0:T(8,128)(2,1)} %broadcast_in_dim.128), calls=%async_computation.3 | async-start | bytes 1572864 | tf_op jit(solution)/shard_map/all_to_all | solution.py:23
  614.6 16.2 %dynamic-slice-start = ((f32[4096]{0:T(1024)}, s32[]{:T(128)}), f32[1024]{0:T(1024)S(1)}, s32[]{:S(2)}) async-start(f32[4096]{0:T(1024)} %param.27, s32[]{:T(128)} %select_n.118), calls=%async_computation.6 | async-start | bytes 8704 | tf_op jit(solution)/shard_map/dynamic_slice | solution.py:180
  624.7 12.8 %all-to-all-start.5 = ((bf16[32,1,32]{2,1,0:T(2,128)(2,1)}), bf16[32,1,32]{2,1,0:T(2,128)(2,1)S(1)}, u32[]{:S(2)}, u32[]{:S(2)}) async-start(bf16[32,1,32]{2,1,0:T(2,128)(2,1)} %broadcast_in_dim.130), calls=%async_computation.5 | async-start | bytes 32768 | tf_op jit(solution)/shard_map/all_to_all | solution.py:23
  639.1 32.3 %all-to-all-start.4 = ((bf16[32,32,1024]{2,1,0:T(8,128)(2,1)}), bf16[32,32,1024]{2,1,0:T(8,128)(2,1)S(1)}, u32[]{:S(2)}, u32[]{:S(2)}) async-start(bf16[32,32,1024]{2,1,0:T(8,128)(2,1)} %broadcast_in_dim.129), calls=%async_computation.4 | async-start | bytes 4194304 | tf_op jit(solution)/shard_map/all_to_all | solution.py:23
  671.9 10.0 %copy-start.2 = (f32[32,1024]{1,0:T(8,128)}, f32[32,1024]{1,0:T(8,128)S(1)}, u32[]{:S(2)}) copy-start(f32[32,1024]{1,0:T(8,128)S(1)} %broadcast_divide_fusion) | copy-start | bytes 393220
  (3 other events, 18.5 us)
where the time goes:
time: 684 us; the launch traced here: 682 us
  waiting for transfers between devices  245 us (36%)
  blocking collectives  159 us (23%)
  matrix products  104 us (15%)
  starting transfers between devices  78.1 us (11%)
  local copies, waits for them, and re-layouts  51.8 us (8%)
  other arithmetic  39.9 us (6%)
    all_to_all x11, waiting for transfers between devices, sent_to_all(): return lax.all_to_all(copies, axis, split_axis=0, concat_axis=0, tiled=True)  108 us
    all_to_all x8, waiting for transfers between devices, sum_at_owner(): lax.all_to_all(split_up(shard, dim, length), axis, 0, 0, tiled=True)  82.5 us
    unnamed x1, blocking collectives  79.5 us
    dot_general x8, matrix products, section_block(): projected = jnp.dot(normed, w_in, preferred_element_type=jnp.float32)  54.2 us
    ppermute x8, waiting for transfers between devices, passed_along(): return lax.ppermute(block, axis, route)  53.9 us
    all_to_all x11, starting transfers between devices, sent_to_all(): return lax.all_to_all(copies, axis, split_axis=0, concat_axis=0, tiled=True)  42.8 us
    dot_general x8, matrix products, section_block(): partial_out = jnp.dot(mixed, out_proj, preferred_element_type=jnp.float32)  38.7 us
    all_gather x1, blocking collectives, shards(): lax.all_gather(support_tokens, ('dp', 'pipe'), axis=0, tiled=True)  36.5 us
  transfers between devices with their start and end apart: 28, of which 27 were waited for; matrix products, arithmetic and copies ran while one was open for 4% of the time, Pallas kernels for 0%

commit v1 on v0

--- a/solution.py
+++ b/solution.py
@@ -10,6 +10,27 @@
 EPISODES = 2
 epsilon = 1e-05
 rotary_base = 500000.0
+
+
+def joined_along(tiles, dim):
+    tiles = jnp.moveaxis(tiles, 0, dim)
+    shape = tiles.shape
+    return tiles.reshape(*shape[:dim], shape[dim] * shape[dim + 1], *shape[dim + 2 :])
+
+
+def doubled(x, axis):
+    length, place = (lax.axis_size(axis), lax.axis_index(axis))
+    pieces, bit = (x[None], 1)
+    while bit < length:
+        other = lax.ppermute(pieces, axis, [(i, i ^ bit) for i in range(length)])
+        low = place & bit == 0
+        pieces = jnp.concatenate([jnp.where(low, pieces, other), jnp.where(low, other, pieces)])
+        bit *= 2
+    return pieces
+
+
+def collect_2(x, axis, dim):
+    return joined_along(doubled(x, axis), dim)
 
 
 def in_order(blocks, dim):
@@ -99,7 +120,7 @@
     table_rows, width = embedding.shape
     column_start = lax.axis_index("tensor") * width
     all_support, all_query, every_sup_len, every_qry_len = (
-        lax.all_gather(support_tokens, ("dp", "pipe"), axis=0, tiled=True),
+        collect_2(support_tokens, ("dp", "pipe"), 0),
         lax.all_gather(query_tokens, ("dp", "pipe"), axis=0, tiled=True),
         lax.all_gather(support_lengths, ("dp", "pipe"), axis=0, tiled=True),
         lax.all_gather(query_lengths, ("dp", "pipe"), axis=0, tiled=True),

time: 684 us -> 664 us (0.971)
  blocking collectives: 159 us -> 121 us
  starting transfers between devices: 78.1 us -> 87.5 us
  waiting for transfers between devices: 245 us -> 252 us
    all_gather x1 -> x0, blocking collectives: 36.5 us -> none  [shards(): lax.all_gather(support_tokens, ('dp', 'pipe'), axis=0, tiled=True)]
    ppermute x0 -> x5, starting transfers between devices: none -> 10.1 us  [doubled(): other = lax.ppermute(pieces, axis, [(i, i ^ bit) for i in range(length)])]
    ppermute x0 -> x5, waiting for transfers between devices: none -> 7.08 us  [doubled(): other = lax.ppermute(pieces, axis, [(i, i ^ bit) for i in range(length)])]
  transfers between devices with their start and end apart: 28 -> 33, of which waited for: 27 -> 31; matrix products, arithmetic and copies ran while one was open for 4% -> 4% of each run, Pallas kernels for 0% -> 0%
where the time goes in v1:
time: 664 us; the launch traced here: 662 us
  waiting for transfers between devices  252 us (38%)
  blocking collectives  121 us (18%)
  matrix products  104 us (16%)
  starting transfers between devices  87.5 us (13%)
  local copies, waits for them, and re-layouts  51.8 us (8%)
  other arithmetic  40.6 us (6%)
    all_to_all x11, waiting for transfers between devices, sent_to_all(): return lax.all_to_all(copies, axis, split_axis=0, concat_axis=0, tiled=True)  108 us
    all_to_all x8, waiting for transfers between devices, sum_at_owner(): lax.all_to_all(split_up(shard, dim, length), axis, 0, 0, tiled=True)  82.5 us
    unnamed x1, blocking collectives  79.4 us
    dot_general x8, matrix products, section_block(): projected = jnp.dot(normed, w_in, preferred_element_type=jnp.float32)  54.2 us
    ppermute x8, waiting for transfers between devices, passed_along(): return lax.ppermute(block, axis, route)  53.8 us
    all_to_all x11, starting transfers between devices, sent_to_all(): return lax.all_to_all(copies, axis, split_axis=0, concat_axis=0, tiled=True)  42.8 us
    dot_general x8, matrix products, section_block(): partial_out = jnp.dot(mixed, out_proj, preferred_element_type=jnp.float32)  38.7 us
    all_gather x1, blocking collectives, shards(): lax.all_gather(query_tokens, ('dp', 'pipe'), axis=0, tiled=True)  32.8 us
  transfers between devices with their start and end apart: 33, of which 31 were waited for; matrix products, arithmetic and copies ran while one was open for 4% of the time, Pallas kernels for 0%

profile of v1, /device:TPU:0, one launch (start us, length us, event | category | flops | bytes accessed | tf_op | source)
XLA Modules:
  0.0 661.5 jit_solution(6167167001249094937)
XLA Ops:
  18.5 32.8 %all-gather = s32[32,1,32]{2,1,0:T(1,128)S(1)} all-gather(s32[1,1,32]{2,1,0:T(1,128)} %bitcast.150), channel_id=1, replica_groups=mesh['dp'=8,'pipe'=4,'tensor'=4] {'dp','pipe'}, dimensions={0}, use_global_device_ids=true | all-gather | bytes 4224 | tf_op jit(solution)/shard_map/all_gather | solution.py:124
  51.7 18.7 %gather_fusion = bf16[3072,1024]{1,0:T(8,128)(2,1)} fusion(bf16[2004,1024]{1,0:T(8,128)(2,1)} %param.21, s32[3072]{0:T(1024)S(1)} %broadcast_clamp_fusion.1), kind=kCustom, calls=%fused_computation | custom fusion | bytes 12595200 | tf_op jit(solution)/shard_map/jit(_take)/gather | solution.py:133
  70.4 7.0 %select_select_fusion = bf16[32,96,1024]{2,1,0:T(8,128)(2,1)} fusion(bf16[32,96,1024]{2,1,0:T(8,128)(2,1)} %bitcast.130, pred[32,96]{1,0:T(8,128)(4,1)S(1)} %get-tuple-element.312, pred[32,96]{1,0:T(8,128)(4,1)S(1)} %get-tuple-element.322), kind=kLoop, calls=%fused_computation.56 | loop fusion | flops 6291456 | bytes 12589056 | tf_op jit(solution)/shard_map/jit(_where)/select_n | solution.py:134
  85.5 79.4 %all-reduce.2 = (s32[64]{0:T(128)S(1)}, s32[32]{0:T(128)S(1)}) all-reduce(s32[64]{0:T(128)S(1)} %dynamic-update-slice, s32[32]{0:T(128)S(1)} %dynamic-update-slice.1), channel_id=1, replica_groups=mesh['dp'=8,'pipe'=4,'tensor'=4] {'dp','pipe'}, use_global_device_ids=true, to_apply=%add | all-reduce | flops 96 | bytes 768
  164.9 11.6 %pad_maximum_fusion = bf16[4096,1536]{1,0:T(8,128)(2,1)} fusion(bf16[4096,256]{1,0:T(8,128)(2,1)S(1)} %bitcast.137, bf16[4096,256]{1,0:T(8,128)(2,1)} %bitcast.138, bf16[4096,1024]{1,0:T(8,128)(2,1)} %bitcast.131), kind=kLoop, calls=%fused_computation.55 | loop fusion | flops 37748736 | bytes 25165824 | tf_op jit(solution)/shard_map/concatenate | solution.py:148
  180.8 409.0 %while.16 = (s32[]{:T(128)}, bf16[96,1024]{1,0:T(8,128)(2,1)S(1)}, s32[]{:T(128)}, f32[1,4096]{1,0:T(1,128)S(1)}, bf16[4096,1536]{1,0:T(8,128)(2,1)}, /*index=5*...) while((s32[]{:T(128)}, bf16[96,1024]{1,0:T(8,128)(2,1)S(1)}, ...), condition=%wide.region_6.7_spmd.clone, body=%wide.region_1.6_spmd.clone.sunk | while | flops 2038168704 | bytes 45535072 | solution.py:200
  188.9 10.1 %all-to-all-done = bf16[4,96,1024]{2,1,0:T(8,128)(2,1)S(1)} async-done(((bf16[4,96,1024]{2,1,0:T(8,128)(2,1)}), bf16[4,96,1024]{2,1,0:T(8,128)(2,1)S(1)}, u32[]{:S(2)}, u32[]{:S(2)}) %all-to-all-start) | async-done | bytes 786464 | tf_op jit(solution)/shard_map/while/body/eval_jaxpr/all_to_all | solution.py:44
  218.0 11.0 %all-to-all-done.1 = bf16[4,96,1024]{2,1,0:T(8,128)(2,1)S(1)} async-done(((bf16[4,96,1024]{2,1,0:T(8,128)(2,1)}), bf16[4,96,1024]{2,1,0:T(8,128)(2,1)S(1)}, u32[]{:S(2)}, u32[]{:S(2)}) %all-to-all-start.1) | async-done | bytes 786464 | tf_op jit(solution)/shard_map/while/body/eval_jaxpr/all_to_all | solution.py:59
  242.4 7.7 %all-to-all-done = bf16[4,96,1024]{2,1,0:T(8,128)(2,1)S(1)} async-done(((bf16[4,96,1024]{2,1,0:T(8,128)(2,1)}), bf16[4,96,1024]{2,1,0:T(8,128)(2,1)S(1)}, u32[]{:S(2)}, u32[]{:S(2)}) %all-to-all-start) | async-done | bytes 786464 | tf_op jit(solution)/shard_map/while/body/eval_jaxpr/all_to_all | solution.py:44
  269.0 9.4 %all-to-all-done.1 = bf16[4,96,1024]{2,1,0:T(8,128)(2,1)S(1)} async-done(((bf16[4,96,1024]{2,1,0:T(8,128)(2,1)}), bf16[4,96,1024]{2,1,0:T(8,128)(2,1)S(1)}, u32[]{:S(2)}, u32[]{:S(2)}) %all-to-all-start.1) | async-done | bytes 786464 | tf_op jit(solution)/shard_map/while/body/eval_jaxpr/all_to_all | solution.py:59
  278.7 6.9 %collective-permute-done = bf16[96,1024]{1,0:T(8,128)(2,1)S(1)} collective-permute-done((bf16[96,1024]{1,0:T(8,128)(2,1)S(1)}, bf16[96,1024]{1,0:T(8,128)(2,1)S(1)}, u32[]{:S(2)}, u32[]{:S(2)}) %collective-permute-start) | collective-permute-done | bytes 196640 | tf_op jit(solution)/shard_map/while/body/eval_jaxpr/ppermute | solution.py:66
  291.9 7.7 %all-to-all-done = bf16[4,96,1024]{2,1,0:T(8,128)(2,1)S(1)} async-done(((bf16[4,96,1024]{2,1,0:T(8,128)(2,1)}), bf16[4,96,1024]{2,1,0:T(8,128)(2,1)S(1)}, u32[]{:S(2)}, u32[]{:S(2)}) %all-to-all-start) | async-done | bytes 786464 | tf_op jit(solution)/shard_map/while/body/eval_jaxpr/all_to_all | solution.py:44
  318.5 9.4 %all-to-all-done.1 = bf16[4,96,1024]{2,1,0:T(8,128)(2,1)S(1)} async-done(((bf16[4,96,1024]{2,1,0:T(8,128)(2,1)}), bf16[4,96,1024]{2,1,0:T(8,128)(2,1)S(1)}, u32[]{:S(2)}, u32[]{:S(2)}) %all-to-all-start.1) | async-done | bytes 786464 | tf_op jit(solution)/shard_map/while/body/eval_jaxpr/all_to_all | solution.py:59
  328.2 6.9 %collective-permute-done = bf16[96,1024]{1,0:T(8,128)(2,1)S(1)} collective-permute-done((bf16[96,1024]{1,0:T(8,128)(2,1)S(1)}, bf16[96,1024]{1,0:T(8,128)(2,1)S(1)}, u32[]{:S(2)}, u32[]{:S(2)}) %collective-permute-start) | collective-permute-done | bytes 196640 | tf_op jit(solution)/shard_map/while/body/eval_jaxpr/ppermute | solution.py:66
  341.3 7.7 %all-to-all-done = bf16[4,96,1024]{2,1,0:T(8,128)(2,1)S(1)} async-done(((bf16[4,96,1024]{2,1,0:T(8,128)(2,1)}), bf16[4,96,1024]{2,1,0:T(8,128)(2,1)S(1)}, u32[]{:S(2)}, u32[]{:S(2)}) %all-to-all-start) | async-done | bytes 786464 | tf_op jit(solution)/shard_map/while/body/eval_jaxpr/all_to_all | solution.py:44
  368.0 9.4 %all-to-all-done.1 = bf16[4,96,1024]{2,1,0:T(8,128)(2,1)S(1)} async-done(((bf16[4,96,1024]{2,1,0:T(8,128)(2,1)}), bf16[4,96,1024]{2,1,0:T(8,128)(2,1)S(1)}, u32[]{:S(2)}, u32[]{:S(2)}) %all-to-all-start.1) | async-done | bytes 786464 | tf_op jit(solution)/shard_map/while/body/eval_jaxpr/all_to_all | solution.py:59
  377.7 6.9 %collective-permute-done = bf16[96,1024]{1,0:T(8,128)(2,1)S(1)} collective-permute-done((bf16[96,1024]{1,0:T(8,128)(2,1)S(1)}, bf16[96,1024]{1,0:T(8,128)(2,1)S(1)}, u32[]{:S(2)}, u32[]{:S(2)}) %collective-permute-start) | collective-permute-done | bytes 196640 | tf_op jit(solution)/shard_map/while/body/eval_jaxpr/ppermute | solution.py:66
  390.8 7.7 %all-to-all-done = bf16[4,96,1024]{2,1,0:T(8,128)(2,1)S(1)} async-done(((bf16[4,96,1024]{2,1,0:T(8,128)(2,1)}), bf16[4,96,1024]{2,1,0:T(8,128)(2,1)S(1)}, u32[]{:S(2)}, u32[]{:S(2)}) %all-to-all-start) | async-done | bytes 786464 | tf_op jit(solution)/shard_map/while/body/eval_jaxpr/all_to_all | solution.py:44
  417.5 10.7 %all-to-all-done.1 = bf16[4,96,1024]{2,1,0:T(8,128)(2,1)S(1)} async-done(((bf16[4,96,1024]{2,1,0:T(8,128)(2,1)}), bf16[4,96,1024]{2,1,0:T(8,128)(2,1)S(1)}, u32[]{:S(2)}, u32[]{:S(2)}) %all-to-all-start.1) | async-done | bytes 786464 | tf_op jit(solution)/shard_map/while/body/eval_jaxpr/all_to_all | solution.py:59
  428.4 6.9 %collective-permute-done = bf16[96,1024]{1,0:T(8,128)(2,1)S(1)} collective-permute-done((bf16[96,1024]{1,0:T(8,128)(2,1)S(1)}, bf16[96,1024]{1,0:T(8,128)(2,1)S(1)}, u32[]{:S(2)}, u32[]{:S(2)}) %collective-permute-start) | collective-permute-done | bytes 196640 | tf_op jit(solution)/shard_map/while/body/eval_jaxpr/ppermute | solution.py:66
  441.6 7.7 %all-to-all-done = bf16[4,96,1024]{2,1,0:T(8,128)(2,1)S(1)} async-done(((bf16[4,96,1024]{2,1,0:T(8,128)(2,1)}), bf16[4,96,1024]{2,1,0:T(8,128)(2,1)S(1)}, u32[]{:S(2)}, u32[]{:S(2)}) %all-to-all-start) | async-done | bytes 786464 | tf_op jit(solution)/shard_map/while/body/eval_jaxpr/all_to_all | solution.py:44
  468.2 13.1 %all-to-all-done.1 = bf16[4,96,1024]{2,1,0:T(8,128)(2,1)S(1)} async-done(((bf16[4,96,1024]{2,1,0:T(8,128)(2,1)}), bf16[4,96,1024]{2,1,0:T(8,128)(2,1)S(1)}, u32[]{:S(2)}, u32[]{:S(2)}) %all-to-all-start.1) | async-done | bytes 786464 | tf_op jit(solution)/shard_map/while/body/eval_jaxpr/all_to_all | solution.py:59
  481.6 6.9 %collective-permute-done = bf16[96,1024]{1,0:T(8,128)(2,1)S(1)} collective-permute-done((bf16[96,1024]{1,0:T(8,128)(2,1)S(1)}, bf16[96,1024]{1,0:T(8,128)(2,1)S(1)}, u32[]{:S(2)}, u32[]{:S(2)}) %collective-permute-start) | collective-permute-done | bytes 196640 | tf_op jit(solution)/shard_map/while/body/eval_jaxpr/ppermute | solution.py:66
  494.8 7.7 %all-to-all-done = bf16[4,96,1024]{2,1,0:T(8,128)(2,1)S(1)} async-done(((bf16[4,96,1024]{2,1,0:T(8,128)(2,1)}), bf16[4,96,1024]{2,1,0:T(8,128)(2,1)S(1)}, u32[]{:S(2)}, u32[]{:S(2)}) %all-to-all-start) | async-done | bytes 786464 | tf_op jit(solution)/shard_map/while/body/eval_jaxpr/all_to_all | solution.py:44
  521.4 10.0 %all-to-all-done.1 = bf16[4,96,1024]{2,1,0:T(8,128)(2,1)S(1)} async-done(((bf16[4,96,1024]{2,1,0:T(8,128)(2,1)}), bf16[4,96,1024]{2,1,0:T(8,128)(2,1)S(1)}, u32[]{:S(2)}, u32[]{:S(2)}) %all-to-all-start.1) | async-done | bytes 786464 | tf_op jit(solution)/shard_map/while/body/eval_jaxpr/all_to_all | solution.py:59
  531.7 6.9 %collective-permute-done = bf16[96,1024]{1,0:T(8,128)(2,1)S(1)} collective-permute-done((bf16[96,1024]{1,0:T(8,128)(2,1)S(1)}, bf16[96,1024]{1,0:T(8,128)(2,1)S(1)}, u32[]{:S(2)}, u32[]{:S(2)}) %collective-permute-start) | collective-permute-done | bytes 196640 | tf_op jit(solution)/shard_map/while/body/eval_jaxpr/ppermute | solution.py:66
  544.8 9.5 %all-to-all-done = bf16[4,96,1024]{2,1,0:T(8,128)(2,1)S(1)} async-done(((bf16[4,96,1024]{2,1,0:T(8,128)(2,1)}), bf16[4,96,1024]{2,1,0:T(8,128)(2,1)S(1)}, u32[]{:S(2)}, u32[]{:S(2)}) %all-to-all-start) | async-done | bytes 786464 | tf_op jit(solution)/shard_map/while/body/eval_jaxpr/all_to_all | solution.py:44
  573.2 9.4 %all-to-all-done.1 = bf16[4,96,1024]{2,1,0:T(8,128)(2,1)S(1)} async-done(((bf16[4,96,1024]{2,1,0:T(8,128)(2,1)}), bf16[4,96,1024]{2,1,0:T(8,128)(2,1)S(1)}, u32[]{:S(2)}, u32[]{:S(2)}) %all-to-all-start.1) | async-done | bytes 786464 | tf_op jit(solution)/shard_map/while/body/eval_jaxpr/all_to_all | solution.py:59
  582.9 6.9 %collective-permute-done = bf16[96,1024]{1,0:T(8,128)(2,1)S(1)} collective-permute-done((bf16[96,1024]{1,0:T(8,128)(2,1)S(1)}, bf16[96,1024]{1,0:T(8,128)(2,1)S(1)}, u32[]{:S(2)}, u32[]{:S(2)}) %collective-permute-start) | collective-permute-done | bytes 196640 | tf_op jit(solution)/shard_map/while/body/eval_jaxpr/ppermute | solution.py:66
  594.5 9.2 %all-to-all-done.3 = bf16[4,96,1024]{2,1,0:T(8,128)(2,1)S(1)} async-done(((bf16[4,96,1024]{2,1,0:T(8,128)(2,1)}), bf16[4,96,1024]{2,1,0:T(8,128)(2,1)S(1)}, u32[]{:S(2)}, u32[]{:S(2)}) %all-to-all-start.3) | async-done | bytes 786464 | tf_op jit(solution)/shard_map/all_to_all | solution.py:44
  623.5 27.6 %all-to-all-done.4 = bf16[32,32,1024]{2,1,0:T(8,128)(2,1)S(1)} async-done(((bf16[32,32,1024]{2,1,0:T(8,128)(2,1)}), bf16[32,32,1024]{2,1,0:T(8,128)(2,1)S(1)}, u32[]{:S(2)}, u32[]{:S(2)}) %all-to-all-start.4) | async-done | bytes 2097184 | tf_op jit(solution)/shard_map/all_to_all | solution.py:44
  652.1 8.9 %psum.7 = f32[1,16]{1,0:T(1,128)S(1)} all-reduce(f32[1,16]{1,0:T(1,128)S(1)} %bitcast.149), channel_id=1, replica_groups=mesh['dp'=8,'pipe'=4,'tensor'=4] {'tensor'}, use_global_device_ids=true, to_apply=%region_13.14 | all-reduce | flops 16 | bytes 128 | tf_op jit(solution)/shard_map/psum | solution.py:229
  (361 shorter events, 265.5 us)
Async XLA Ops:
  0.6 3.9 collective-permute-start.1
  5.2 5.1 collective-permute-start.2
  11.6 3.7 collective-permute-start.4
  15.3 36.1 %collective-permute-start.5 = (s32[16,2,32]{2,1,0:T(2,128)S(1)}, s32[16,2,32]{2,1,0:T(2,128)S(1)}, u32[]{:S(2)}, u32[]{:S(2)}) collective-permute-start(s32[16,2,32]{2,1,0:T(2,128)S(1)} %pad_add_fusion.2), channel_id=1, source_target_pairs={{0,64},{4,68},{8,72},{12,76},{16,80},{20,84},{24,88},{28,92},{32,9... | collective-permute-start | bytes 12296 | tf_op jit(solution)/shard_map/ppermute | solution.py:25
  77.4 99.1 %all-to-all-start.2 = ((bf16[32,96,1024]{2,1,0:T(8,128)(2,1)}), bf16[32,96,1024]{2,1,0:T(8,128)(2,1)}, u32[]{:S(2)}, u32[]{:S(2)}) async-start(bf16[32,96,1024]{2,1,0:T(8,128)(2,1)} %select_select_fusion), calls=%async_computation.2 | async-start | bytes 12582912 | tf_op jit(solution)/shard_map/all_to_all | solution.py:135
  181.8 17.2 %all-to-all-start = ((bf16[4,96,1024]{2,1,0:T(8,128)(2,1)}), bf16[4,96,1024]{2,1,0:T(8,128)(2,1)S(1)}, u32[]{:S(2)}, u32[]{:S(2)}) async-start(bf16[4,96,1024]{2,1,0:T(8,128)(2,1)} %broadcast_in_dim.173), calls=%async_computation | async-start | bytes 1572864 | tf_op jit(solution)/shard_map/while/body/eval_jaxpr/all_to_all | solution.py:44
  214.4 14.5 %all-to-all-start.1 = ((bf16[4,96,1024]{2,1,0:T(8,128)(2,1)}), bf16[4,96,1024]{2,1,0:T(8,128)(2,1)S(1)}, u32[]{:S(2)}, u32[]{:S(2)}) async-start(bf16[4,96,1024]{2,1,0:T(8,128)(2,1)} %bitcast.124), calls=%async_computation.1 | async-start | bytes 1572864 | tf_op jit(solution)/shard_map/while/body/eval_jaxpr/all_to_all | solution.py:59
  229.1 6.9 %collective-permute-start = (bf16[96,1024]{1,0:T(8,128)(2,1)S(1)}, bf16[96,1024]{1,0:T(8,128)(2,1)S(1)}, u32[]{:S(2)}, u32[]{:S(2)}) collective-permute-start(bf16[96,1024]{1,0:T(8,128)(2,1)S(1)} %fusion.89), channel_id=1, source_target_pairs={{12,0},{0,4},{4,8},{8,12},{13,1},{1,5},{5,9},{9,13},{14,2},{2,6},{... | collective-permute-start | bytes 589832 | tf_op jit(solution)/shard_map/while/body/eval_jaxpr/ppermute | solution.py:66
  237.1 13.0 %all-to-all-start = ((bf16[4,96,1024]{2,1,0:T(8,128)(2,1)}), bf16[4,96,1024]{2,1,0:T(8,128)(2,1)S(1)}, u32[]{:S(2)}, u32[]{:S(2)}) async-start(bf16[4,96,1024]{2,1,0:T(8,128)(2,1)} %broadcast_in_dim.173), calls=%async_computation | async-start | bytes 1572864 | tf_op jit(solution)/shard_map/while/body/eval_jaxpr/all_to_all | solution.py:44
  265.5 13.0 %all-to-all-start.1 = ((bf16[4,96,1024]{2,1,0:T(8,128)(2,1)}), bf16[4,96,1024]{2,1,0:T(8,128)(2,1)S(1)}, u32[]{:S(2)}, u32[]{:S(2)}) async-start(bf16[4,96,1024]{2,1,0:T(8,128)(2,1)} %bitcast.124), calls=%async_computation.1 | async-start | bytes 1572864 | tf_op jit(solution)/shard_map/while/body/eval_jaxpr/all_to_all | solution.py:59
  278.6 6.9 %collective-permute-start = (bf16[96,1024]{1,0:T(8,128)(2,1)S(1)}, bf16[96,1024]{1,0:T(8,128)(2,1)S(1)}, u32[]{:S(2)}, u32[]{:S(2)}) collective-permute-start(bf16[96,1024]{1,0:T(8,128)(2,1)S(1)} %fusion.89), channel_id=1, source_target_pairs={{12,0},{0,4},{4,8},{8,12},{13,1},{1,5},{5,9},{9,13},{14,2},{2,6},{... | collective-permute-start | bytes 589832 | tf_op jit(solution)/shard_map/while/body/eval_jaxpr/ppermute | solution.py:66
  286.6 13.0 %all-to-all-start = ((bf16[4,96,1024]{2,1,0:T(8,128)(2,1)}), bf16[4,96,1024]{2,1,0:T(8,128)(2,1)S(1)}, u32[]{:S(2)}, u32[]{:S(2)}) async-start(bf16[4,96,1024]{2,1,0:T(8,128)(2,1)} %broadcast_in_dim.173), calls=%async_computation | async-start | bytes 1572864 | tf_op jit(solution)/shard_map/while/body/eval_jaxpr/all_to_all | solution.py:44
  314.9 13.0 %all-to-all-start.1 = ((bf16[4,96,1024]{2,1,0:T(8,128)(2,1)}), bf16[4,96,1024]{2,1,0:T(8,128)(2,1)S(1)}, u32[]{:S(2)}, u32[]{:S(2)}) async-start(bf16[4,96,1024]{2,1,0:T(8,128)(2,1)} %bitcast.124), calls=%async_computation.1 | async-start | bytes 1572864 | tf_op jit(solution)/shard_map/while/body/eval_jaxpr/all_to_all | solution.py:59
  328.1 6.9 %collective-permute-start = (bf16[96,1024]{1,0:T(8,128)(2,1)S(1)}, bf16[96,1024]{1,0:T(8,128)(2,1)S(1)}, u32[]{:S(2)}, u32[]{:S(2)}) collective-permute-start(bf16[96,1024]{1,0:T(8,128)(2,1)S(1)} %fusion.89), channel_id=1, source_target_pairs={{12,0},{0,4},{4,8},{8,12},{13,1},{1,5},{5,9},{9,13},{14,2},{2,6},{... | collective-permute-start | bytes 589832 | tf_op jit(solution)/shard_map/while/body/eval_jaxpr/ppermute | solution.py:66
  336.1 13.0 %all-to-all-start = ((bf16[4,96,1024]{2,1,0:T(8,128)(2,1)}), bf16[4,96,1024]{2,1,0:T(8,128)(2,1)S(1)}, u32[]{:S(2)}, u32[]{:S(2)}) async-start(bf16[4,96,1024]{2,1,0:T(8,128)(2,1)} %broadcast_in_dim.173), calls=%async_computation | async-start | bytes 1572864 | tf_op jit(solution)/shard_map/while/body/eval_jaxpr/all_to_all | solution.py:44
  364.4 13.0 %all-to-all-start.1 = ((bf16[4,96,1024]{2,1,0:T(8,128)(2,1)}), bf16[4,96,1024]{2,1,0:T(8,128)(2,1)S(1)}, u32[]{:S(2)}, u32[]{:S(2)}) async-start(bf16[4,96,1024]{2,1,0:T(8,128)(2,1)} %bitcast.124), calls=%async_computation.1 | async-start | bytes 1572864 | tf_op jit(solution)/shard_map/while/body/eval_jaxpr/all_to_all | solution.py:59
  377.6 6.9 %collective-permute-start = (bf16[96,1024]{1,0:T(8,128)(2,1)S(1)}, bf16[96,1024]{1,0:T(8,128)(2,1)S(1)}, u32[]{:S(2)}, u32[]{:S(2)}) collective-permute-start(bf16[96,1024]{1,0:T(8,128)(2,1)S(1)} %fusion.89), channel_id=1, source_target_pairs={{12,0},{0,4},{4,8},{8,12},{13,1},{1,5},{5,9},{9,13},{14,2},{2,6},{... | collective-permute-start | bytes 589832 | tf_op jit(solution)/shard_map/while/body/eval_jaxpr/ppermute | solution.py:66
  385.6 13.0 %all-to-all-start = ((bf16[4,96,1024]{2,1,0:T(8,128)(2,1)}), bf16[4,96,1024]{2,1,0:T(8,128)(2,1)S(1)}, u32[]{:S(2)}, u32[]{:S(2)}) async-start(bf16[4,96,1024]{2,1,0:T(8,128)(2,1)} %broadcast_in_dim.173), calls=%async_computation | async-start | bytes 1572864 | tf_op jit(solution)/shard_map/while/body/eval_jaxpr/all_to_all | solution.py:44
  413.9 14.2 %all-to-all-start.1 = ((bf16[4,96,1024]{2,1,0:T(8,128)(2,1)}), bf16[4,96,1024]{2,1,0:T(8,128)(2,1)S(1)}, u32[]{:S(2)}, u32[]{:S(2)}) async-start(bf16[4,96,1024]{2,1,0:T(8,128)(2,1)} %bitcast.124), calls=%async_computation.1 | async-start | bytes 1572864 | tf_op jit(solution)/shard_map/while/body/eval_jaxpr/all_to_all | solution.py:59
  428.4 6.9 %collective-permute-start = (bf16[96,1024]{1,0:T(8,128)(2,1)S(1)}, bf16[96,1024]{1,0:T(8,128)(2,1)S(1)}, u32[]{:S(2)}, u32[]{:S(2)}) collective-permute-start(bf16[96,1024]{1,0:T(8,128)(2,1)S(1)} %fusion.89), channel_id=1, source_target_pairs={{12,0},{0,4},{4,8},{8,12},{13,1},{1,5},{5,9},{9,13},{14,2},{2,6},{... | collective-permute-start | bytes 589832 | tf_op jit(solution)/shard_map/while/body/eval_jaxpr/ppermute | solution.py:66
  436.3 13.0 %all-to-all-start = ((bf16[4,96,1024]{2,1,0:T(8,128)(2,1)}), bf16[4,96,1024]{2,1,0:T(8,128)(2,1)S(1)}, u32[]{:S(2)}, u32[]{:S(2)}) async-start(bf16[4,96,1024]{2,1,0:T(8,128)(2,1)} %broadcast_in_dim.173), calls=%async_computation | async-start | bytes 1572864 | tf_op jit(solution)/shard_map/while/body/eval_jaxpr/all_to_all | solution.py:44
  464.7 16.6 %all-to-all-start.1 = ((bf16[4,96,1024]{2,1,0:T(8,128)(2,1)}), bf16[4,96,1024]{2,1,0:T(8,128)(2,1)S(1)}, u32[]{:S(2)}, u32[]{:S(2)}) async-start(bf16[4,96,1024]{2,1,0:T(8,128)(2,1)} %bitcast.124), calls=%async_computation.1 | async-start | bytes 1572864 | tf_op jit(solution)/shard_map/while/body/eval_jaxpr/all_to_all | solution.py:59
  481.5 6.9 %collective-permute-start = (bf16[96,1024]{1,0:T(8,128)(2,1)S(1)}, bf16[96,1024]{1,0:T(8,128)(2,1)S(1)}, u32[]{:S(2)}, u32[]{:S(2)}) collective-permute-start(bf16[96,1024]{1,0:T(8,128)(2,1)S(1)} %fusion.89), channel_id=1, source_target_pairs={{12,0},{0,4},{4,8},{8,12},{13,1},{1,5},{5,9},{9,13},{14,2},{2,6},{... | collective-permute-start | bytes 589832 | tf_op jit(solution)/shard_map/while/body/eval_jaxpr/ppermute | solution.py:66
  489.5 13.0 %all-to-all-start = ((bf16[4,96,1024]{2,1,0:T(8,128)(2,1)}), bf16[4,96,1024]{2,1,0:T(8,128)(2,1)S(1)}, u32[]{:S(2)}, u32[]{:S(2)}) async-start(bf16[4,96,1024]{2,1,0:T(8,128)(2,1)} %broadcast_in_dim.173), calls=%async_computation | async-start | bytes 1572864 | tf_op jit(solution)/shard_map/while/body/eval_jaxpr/all_to_all | solution.py:44
  517.9 13.5 %all-to-all-start.1 = ((bf16[4,96,1024]{2,1,0:T(8,128)(2,1)}), bf16[4,96,1024]{2,1,0:T(8,128)(2,1)S(1)}, u32[]{:S(2)}, u32[]{:S(2)}) async-start(bf16[4,96,1024]{2,1,0:T(8,128)(2,1)} %bitcast.124), calls=%async_computation.1 | async-start | bytes 1572864 | tf_op jit(solution)/shard_map/while/body/eval_jaxpr/all_to_all | solution.py:59
  531.6 6.9 %collective-permute-start = (bf16[96,1024]{1,0:T(8,128)(2,1)S(1)}, bf16[96,1024]{1,0:T(8,128)(2,1)S(1)}, u32[]{:S(2)}, u32[]{:S(2)}) collective-permute-start(bf16[96,1024]{1,0:T(8,128)(2,1)S(1)} %fusion.89), channel_id=1, source_target_pairs={{12,0},{0,4},{4,8},{8,12},{13,1},{1,5},{5,9},{9,13},{14,2},{2,6},{... | collective-permute-start | bytes 589832 | tf_op jit(solution)/shard_map/while/body/eval_jaxpr/ppermute | solution.py:66
  539.5 14.7 %all-to-all-start = ((bf16[4,96,1024]{2,1,0:T(8,128)(2,1)}), bf16[4,96,1024]{2,1,0:T(8,128)(2,1)S(1)}, u32[]{:S(2)}, u32[]{:S(2)}) async-start(bf16[4,96,1024]{2,1,0:T(8,128)(2,1)} %broadcast_in_dim.173), calls=%async_computation | async-start | bytes 1572864 | tf_op jit(solution)/shard_map/while/body/eval_jaxpr/all_to_all | solution.py:44
  569.7 13.0 %all-to-all-start.1 = ((bf16[4,96,1024]{2,1,0:T(8,128)(2,1)}), bf16[4,96,1024]{2,1,0:T(8,128)(2,1)S(1)}, u32[]{:S(2)}, u32[]{:S(2)}) async-start(bf16[4,96,1024]{2,1,0:T(8,128)(2,1)} %bitcast.124), calls=%async_computation.1 | async-start | bytes 1572864 | tf_op jit(solution)/shard_map/while/body/eval_jaxpr/all_to_all | solution.py:59
  582.8 6.9 %collective-permute-start = (bf16[96,1024]{1,0:T(8,128)(2,1)S(1)}, bf16[96,1024]{1,0:T(8,128)(2,1)S(1)}, u32[]{:S(2)}, u32[]{:S(2)}) collective-permute-start(bf16[96,1024]{1,0:T(8,128)(2,1)S(1)} %fusion.89), channel_id=1, source_target_pairs={{12,0},{0,4},{4,8},{8,12},{13,1},{1,5},{5,9},{9,13},{14,2},{2,6},{... | collective-permute-start | bytes 589832 | tf_op jit(solution)/shard_map/while/body/eval_jaxpr/ppermute | solution.py:66
  590.8 13.0 %all-to-all-start.3 = ((bf16[4,96,1024]{2,1,0:T(8,128)(2,1)}), bf16[4,96,1024]{2,1,0:T(8,128)(2,1)S(1)}, u32[]{:S(2)}, u32[]{:S(2)}) async-start(bf16[4,96,1024]{2,1,0:T(8,128)(2,1)} %broadcast_in_dim.132), calls=%async_computation.3 | async-start | bytes 1572864 | tf_op jit(solution)/shard_map/all_to_all | solution.py:44
  604.3 12.8 %all-to-all-start.5 = ((bf16[32,1,32]{2,1,0:T(2,128)(2,1)}), bf16[32,1,32]{2,1,0:T(2,128)(2,1)S(1)}, u32[]{:S(2)}, u32[]{:S(2)}) async-start(bf16[32,1,32]{2,1,0:T(2,128)(2,1)} %broadcast_in_dim.134), calls=%async_computation.5 | async-start | bytes 32768 | tf_op jit(solution)/shard_map/all_to_all | solution.py:44
  618.8 32.3 %all-to-all-start.4 = ((bf16[32,32,1024]{2,1,0:T(8,128)(2,1)}), bf16[32,32,1024]{2,1,0:T(8,128)(2,1)S(1)}, u32[]{:S(2)}, u32[]{:S(2)}) async-start(bf16[32,32,1024]{2,1,0:T(8,128)(2,1)} %broadcast_in_dim.133), calls=%async_computation.4 | async-start | bytes 4194304 | tf_op jit(solution)/shard_map/all_to_all | solution.py:44
  (8 other events, 545.7 us)
